TPU v7x, 32 devices: a whole 2x2x4 slice. The times are simulated.
32 devices in a mesh: freq: 4 (over y, x), rows: 8 (over z, core).
Axes of the slice: x: 2, y: 2, z: 4, core: 2. Of those that a mesh axis runs over, the one named last changes fastest.
Arguments:
- coupling: bfloat16 [8192, 8192], P('rows'), may hold values from -1 to 1
- delays: int32 [8192, 8192], P('rows'), may hold values from 0 to 63
- freq_index: int32 [4], P('freq'), parts along dimension 0, may hold values from 0 to 255
- initial: float32 [4, 2, 8192], P('freq', None, 'rows'), parts along dimension 0, may hold values from -6 to 6
Outputs:
- eigvector: float32 [4, 2, 8192], P('freq', None, 'rows'), parts along dimension 0
- eigvalue: float32 [4, 2], P('freq'), parts along dimension 0
There are 4 independent parts, one for each index of `freq`. A program takes and returns all parts, laid end to end along the dimension named above; an argument that names none is the same for every part. Nothing has to cross between parts.
All inputs are finite; a program needn't handle non-finite values.
Results may differ from a plain program's by a relative error of at most 0.0003.
Values sent between devices are 32-bit elements; how exact they have to be, the bound alone decides.
No kernel may reach another device: no remote copies, remote signals or barrier semaphores. Data moves between devices by JAX's collectives and lax.ppermute only.
A program may use at most 192 MiB of HBM per device.

v0:
```python
import math
import jax
import jax.numpy as jnp
from jax import lax
from jax.sharding import PartitionSpec as P

N = 8192
FTOTAL = 256
ITERS = 4
EPS = 1e-06


def build_operator(coupling, delays, which_freq):
    step_count = which_freq + 1
    residue = jnp.remainder(step_count * delays, 2 * FTOTAL)
    phase_angle = residue.astype(jnp.float32) * (math.pi / FTOTAL)
    weights = coupling.astype(jnp.float32)
    real_part = -weights * jnp.cos(phase_angle)
    imag_part = weights * jnp.sin(phase_angle)
    angular = step_count.astype(jnp.float32) * (math.pi / FTOTAL)
    return (real_part, imag_part, angular)


def product(real_part, imag_part, angular, gathered, own_rows):
    real_prod = jnp.dot(
        real_part, gathered.T, precision=lax.Precision.HIGHEST, preferred_element_type=jnp.float32
    )
    imag_prod = jnp.dot(
        imag_part, gathered.T, precision=lax.Precision.HIGHEST, preferred_element_type=jnp.float32
    )
    new_real = real_prod[:, 0] - imag_prod[:, 1] - angular * own_rows[1]
    new_imag = real_prod[:, 1] + imag_prod[:, 0] + angular * own_rows[0]
    return jnp.stack([new_real, new_imag], axis=0)


def power(coupling, delays, indices, first):
    real_all, imag_all, angular_all = lax.map(
        lambda which: build_operator(coupling, delays, which), indices
    )
    iterate = first
    previous_whole = first
    whole_iterate = first
    divisor = jnp.ones((first.shape[0], 1, 1), jnp.float32)
    for sweep in range(ITERS + 1):
        whole_iterate = lax.all_gather(iterate, "rows", axis=2, tiled=True)
        squares = jnp.sum(whole_iterate * whole_iterate, axis=(1, 2))
        divisor = jnp.sqrt(squares / N + EPS)[:, None, None]
        if sweep < ITERS:
            normed = iterate / divisor
            previous_whole = whole_iterate / divisor
            iterate = lax.map(
                lambda packed: product(packed[0], packed[1], packed[2], packed[3], packed[4]),
                (real_all, imag_all, angular_all, previous_whole, normed),
            )
    dot_real = jnp.sum(
        previous_whole[:, 0] * whole_iterate[:, 0] + previous_whole[:, 1] * whole_iterate[:, 1],
        axis=1,
    )
    dot_imag = jnp.sum(
        previous_whole[:, 0] * whole_iterate[:, 1] - previous_whole[:, 1] * whole_iterate[:, 0],
        axis=1,
    )
    result = iterate / divisor
    estimate = jnp.stack([dot_real, dot_imag], axis=1) / N
    return (result, estimate)


def shards(coupling, delays, freq_index, initial):

    def visit(carry, packed):
        which_freq, first = packed
        result, estimate = power(coupling, delays, which_freq[None], first[None])
        return (carry, (result[0], estimate[0]))

    unused, outputs = lax.scan(visit, jnp.int32(0), (freq_index, initial))
    eigvector, eigvalue = outputs
    return (eigvector, eigvalue)


def solution(mesh):
    return jax.shard_map(
        shards,
        mesh=mesh,
        in_specs=(P("rows", None), P("rows", None), P("freq"), P("freq", None, "rows")),
        out_specs=(P("freq", None, "rows"), P("freq", None)),
        check_vma=False,
    )
```

profile of v0, /device:TPU:0, one launch (start us, length us, event | category | flops | bytes accessed | tf_op | source)
XLA Modules:
  0.0 478.9 jit_solution(772224042721452039)
XLA Ops:
  1.3 15.9 %all_gather.20 = f32[1,2,8192]{2,1,0:T(2,128)S(1)} all-gather(f32[1,2,1024]{2,1,0:T(2,128)} %param.7), channel_id=1, replica_groups=mesh['freq'=4,'rows'=8] {'rows'}, dimensions={2}, use_global_device_ids=true | all-gather | bytes 73728 | tf_op jit(solution)/shard_map/while/body/eval_jaxpr/all_gather | solution.py:45
  17.2 0.7 multiply_reduce_fusion.4
  18.5 0.7 broadcast_divide_fusion.4
  19.3 138.6 %fusion = (f32[1024,8192]{1,0:T(8,128)}, f32[1024,8192]{1,0:T(8,128)}) fusion(bf16[1024,8192]{1,0:T(8,128)(2,1)} %param.4, s32[1024,8192]{1,0:T(8,128)} %param.5, s32[]{:T(128)} %bitcast), kind=kLoop, calls=%fused_computation.5 | loop fusion | flops 150994944 | bytes 117440512 | tf_op jit(solution)/shard_map/while/body/eval_jaxpr/while/body/eval_jaxpr/mul | solution.py:18
  157.8 31.9 %fusion.6 = f32[1024,2]{0,1:T(2,128)S(1)} fusion(f32[1024,8192]{1,0:T(8,128)} %get-tuple-element.181, f32[1,2,8192]{2,1,0:T(2,128)S(1)} %all_gather.20, f32[]{:T(128)S(6)} %sqrt.25), kind=kOutput, calls=%fused_computation.11 | convolution fusion | flops 201342976 | bytes 33628164 | tf_op jit(solution)/shard_map/while/body/eval_jaxpr/while/body/eval_jaxpr/dot_general | solution.py:25
  189.7 32.0 %fusion.4 = f32[1024,2]{0,1:T(2,128)S(1)} fusion(f32[1024,8192]{1,0:T(8,128)} %get-tuple-element.182, f32[1,2,8192]{2,1,0:T(2,128)S(1)} %all_gather.20, f32[]{:T(128)S(6)} %sqrt.25), kind=kOutput, calls=%fused_computation.9 | convolution fusion | flops 201342976 | bytes 33628164 | tf_op jit(solution)/shard_map/while/body/eval_jaxpr/while/body/eval_jaxpr/dot_general | solution.py:28
  221.8 14.0 %all-gather = f32[2,8192]{1,0:T(2,128)S(1)} all-gather(f32[2,1024]{1,0:T(2,128)S(1)} %pad_maximum_fusion), channel_id=2, replica_groups=mesh['freq'=4,'rows'=8] {'rows'}, dimensions={1}, use_global_device_ids=true | all-gather | bytes 73728 | tf_op jit(solution)/shard_map/while/body/eval_jaxpr/all_gather | solution.py:45
  235.8 0.7 multiply_reduce_fusion.2
  237.1 32.1 %fusion.8 = f32[1024,2]{0,1:T(2,128)S(1)} fusion(f32[1024,8192]{1,0:T(8,128)} %get-tuple-element.181, f32[2,8192]{1,0:T(2,128)S(1)} %all-gather, f32[]{:T(128)S(6)} %sqrt.26), kind=kOutput, calls=%fused_computation.66 | convolution fusion | flops 201342976 | bytes 33628164 | tf_op jit(solution)/shard_map/while/body/eval_jaxpr/while/body/eval_jaxpr/dot_general | solution.py:25
  269.2 31.9 %fusion.9 = f32[1024,2]{0,1:T(2,128)S(1)} fusion(f32[1024,8192]{1,0:T(8,128)} %get-tuple-element.182, f32[2,8192]{1,0:T(2,128)S(1)} %all-gather, f32[]{:T(128)S(6)} %sqrt.26), kind=kOutput, calls=%fused_computation.67 | convolution fusion | flops 201342976 | bytes 33628164 | tf_op jit(solution)/shard_map/while/body/eval_jaxpr/while/body/eval_jaxpr/dot_general | solution.py:28
  301.2 14.0 %all-gather.1 = f32[2,8192]{1,0:T(2,128)S(1)} all-gather(f32[2,1024]{1,0:T(2,128)S(1)} %pad_maximum_fusion.1), channel_id=3, replica_groups=mesh['freq'=4,'rows'=8] {'rows'}, dimensions={1}, use_global_device_ids=true | all-gather | bytes 73728 | tf_op jit(solution)/shard_map/while/body/eval_jaxpr/all_gather | solution.py:45
  315.1 0.7 multiply_reduce_fusion.1
  316.5 32.3 %fusion.10 = f32[1024,2]{0,1:T(2,128)S(1)} fusion(f32[1024,8192]{1,0:T(8,128)} %get-tuple-element.181, f32[2,8192]{1,0:T(2,128)S(1)} %all-gather.1, f32[]{:T(128)S(6)} %sqrt.27), kind=kOutput, calls=%fused_computation.68 | convolution fusion | flops 201342976 | bytes 33628164 | tf_op jit(solution)/shard_map/while/body/eval_jaxpr/while/body/eval_jaxpr/dot_general | solution.py:25
  348.8 31.9 %fusion.11 = f32[1024,2]{0,1:T(2,128)S(1)} fusion(f32[1024,8192]{1,0:T(8,128)} %get-tuple-element.182, f32[2,8192]{1,0:T(2,128)S(1)} %all-gather.1, f32[]{:T(128)S(6)} %sqrt.27), kind=kOutput, calls=%fused_computation.69 | convolution fusion | flops 201342976 | bytes 33628164 | tf_op jit(solution)/shard_map/while/body/eval_jaxpr/while/body/eval_jaxpr/dot_general | solution.py:28
  380.8 14.0 %all-gather.2 = f32[2,8192]{1,0:T(2,128)S(1)} all-gather(f32[2,1024]{1,0:T(2,128)S(1)} %pad_maximum_fusion.2), channel_id=4, replica_groups=mesh['freq'=4,'rows'=8] {'rows'}, dimensions={1}, use_global_device_ids=true | all-gather | bytes 73728 | tf_op jit(solution)/shard_map/while/body/eval_jaxpr/all_gather | solution.py:45
  394.8 0.7 multiply_reduce_fusion
  396.1 32.0 %fusion.13 = f32[1024,2]{0,1:T(2,128)S(1)} fusion(f32[1024,8192]{1,0:T(8,128)} %get-tuple-element.182, f32[2,8192]{1,0:T(2,128)S(1)} %all-gather.2, f32[]{:T(128)S(6)} %sqrt.28), kind=kOutput, calls=%fused_computation.71 | convolution fusion | flops 201342976 | bytes 33628164 | tf_op jit(solution)/shard_map/while/body/eval_jaxpr/while/body/eval_jaxpr/dot_general | solution.py:28
  428.2 31.9 %fusion.12 = f32[1024,2]{0,1:T(2,128)S(1)} fusion(f32[1024,8192]{1,0:T(8,128)} %get-tuple-element.181, f32[2,8192]{1,0:T(2,128)S(1)} %all-gather.2, f32[]{:T(128)S(6)} %sqrt.28), kind=kOutput, calls=%fused_computation.70 | convolution fusion | flops 201342976 | bytes 33628164 | tf_op jit(solution)/shard_map/while/body/eval_jaxpr/while/body/eval_jaxpr/dot_general | solution.py:25
  460.2 14.0 %all-gather.3 = f32[2,8192]{1,0:T(2,128)S(1)} all-gather(f32[2,1024]{1,0:T(2,128)S(1)} %pad_maximum_fusion.3), channel_id=5, replica_groups=mesh['freq'=4,'rows'=8] {'rows'}, dimensions={1}, use_global_device_ids=true | all-gather | bytes 73728 | tf_op jit(solution)/shard_map/while/body/eval_jaxpr/all_gather | solution.py:45
  474.2 0.7 multiply_reduce_fusion.3
  475.5 0.6 maximum_divide_fusion.3
  476.1 0.8 add_reduce_fusion
  476.9 1.8 maximum_multiply_fusion
  (16 shorter events, 0.3 us)
where the time goes:
time: 486 us; the launch traced here: 479 us
  matrix products  256 us (53%)
  other arithmetic  146 us (30%)
  blocking collectives  71.9 us (15%)
  between operations  5.07 us (1%)
    mul x1, other arithmetic, build_operator(): real_part = -weights * jnp.cos(phase_angle)  139 us
    dot_general x4, matrix products, product(): jnp.dot(real_part, gathered.T, precision=lax.Precision.HIGHEST, preferred...  128 us
    dot_general x4, matrix products, product(): jnp.dot(imag_part, gathered.T, precision=lax.Precision.HIGHEST, preferred...  128 us
    all_gather x5, blocking collectives, power(): whole_iterate = lax.all_gather(iterate, 'rows', axis=2, tiled=True)  71.9 us

commit v1 on v0

--- a/solution.py
+++ b/solution.py
@@ -42,7 +42,8 @@
     whole_iterate = first
     divisor = jnp.ones((first.shape[0], 1, 1), jnp.float32)
     for sweep in range(ITERS + 1):
-        whole_iterate = lax.all_gather(iterate, "rows", axis=2, tiled=True)
+        shards_2 = lax.all_gather(iterate, "rows", axis=0, tiled=False)
+        whole_iterate = jnp.concatenate(shards_2, axis=2)
         squares = jnp.sum(whole_iterate * whole_iterate, axis=(1, 2))
         divisor = jnp.sqrt(squares / N + EPS)[:, None, None]
         if sweep < ITERS:

time: 486 us -> 485 us (level)
  no operation moved by 1% of the time
where the time goes in v1:
time: 485 us; the launch traced here: 478 us
  matrix products  255 us (53%)
  other arithmetic  146 us (30%)
  blocking collectives  71.9 us (15%)
  between operations  5.1 us (1%)
    mul x1, other arithmetic, build_operator(): real_part = -weights * jnp.cos(phase_angle)  139 us
    dot_general x4, matrix products, product(): jnp.dot(imag_part, gathered.T, precision=lax.Precision.HIGHEST, preferred...  128 us
    dot_general x4, matrix products, product(): jnp.dot(real_part, gathered.T, precision=lax.Precision.HIGHEST, preferred...  127 us
    all_gather x5, blocking collectives, power(): shards_2 = lax.all_gather(iterate, 'rows', axis=0, tiled=False)  71.9 us

profile of v1, /device:TPU:0, one launch (start us, length us, event | category | flops | bytes accessed | tf_op | source)
XLA Modules:
  0.0 478.0 jit_solution(2556770175705546833)
XLA Ops:
  1.3 15.9 %all-gather = f32[8,2,1024]{2,1,0:T(2,128)S(1)} all-gather(f32[1,2,1024]{2,1,0:T(2,128)} %param.7), channel_id=2, replica_groups=mesh['freq'=4,'rows'=8] {'rows'}, dimensions={0}, use_global_device_ids=true | all-gather | bytes 73728 | tf_op jit(solution)/shard_map/while/body/eval_jaxpr/all_gather | solution.py:45
  17.2 0.7 multiply_reduce_fusion.3
  18.6 0.7 broadcast_divide_fusion.4
  19.3 138.6 %fusion = (f32[1024,8192]{1,0:T(8,128)}, f32[1024,8192]{1,0:T(8,128)}) fusion(bf16[1024,8192]{1,0:T(8,128)(2,1)} %param.4, s32[1024,8192]{1,0:T(8,128)} %param.5, s32[]{:T(128)} %bitcast), kind=kLoop, calls=%fused_computation.5 | loop fusion | flops 150994944 | bytes 117440512 | tf_op jit(solution)/shard_map/while/body/eval_jaxpr/while/body/eval_jaxpr/mul | solution.py:18
  157.8 31.7 %fusion.5 = f32[1024,2]{0,1:T(2,128)S(1)} fusion(f32[1024,8192]{1,0:T(8,128)} %get-tuple-element.181, f32[2,8192]{1,0:T(2,128)S(1)} %bitcast.116), kind=kOutput, calls=%fused_computation.63 | convolution fusion | flops 201326592 | bytes 33628160 | tf_op jit(solution)/shard_map/while/body/eval_jaxpr/while/body/eval_jaxpr/dot_general | solution.py:25
  189.6 31.9 %fusion.6 = f32[1024,2]{0,1:T(2,128)S(1)} fusion(f32[1024,8192]{1,0:T(8,128)} %get-tuple-element.182, f32[2,8192]{1,0:T(2,128)S(1)} %bitcast.117), kind=kOutput, calls=%fused_computation.64 | convolution fusion | flops 201326592 | bytes 33628160 | tf_op jit(solution)/shard_map/while/body/eval_jaxpr/while/body/eval_jaxpr/dot_general | solution.py:28
  221.6 14.0 %all-gather.5 = f32[8,2,1024]{2,1,0:T(2,128)S(1)} all-gather(f32[1,2,1024]{2,1,0:T(2,128)S(1)} %maximum_bitcast_fusion), channel_id=3, replica_groups=mesh['freq'=4,'rows'=8] {'rows'}, dimensions={0}, use_global_device_ids=true | all-gather | bytes 73728 | tf_op jit(solution)/shard_map/while/body/eval_jaxpr/all_gather | solution.py:45
  235.6 0.7 multiply_reduce_fusion.2
  237.0 32.0 %fusion.8 = f32[1024,2]{0,1:T(2,128)S(1)} fusion(f32[1024,8192]{1,0:T(8,128)} %get-tuple-element.182, f32[2,8192]{1,0:T(2,128)S(1)} %bitcast.118), kind=kOutput, calls=%fused_computation.66 | convolution fusion | flops 201326592 | bytes 33628160 | tf_op jit(solution)/shard_map/while/body/eval_jaxpr/while/body/eval_jaxpr/dot_general | solution.py:28
  268.9 31.7 %fusion.7 = f32[1024,2]{0,1:T(2,128)S(1)} fusion(f32[1024,8192]{1,0:T(8,128)} %get-tuple-element.181, f32[2,8192]{1,0:T(2,128)S(1)} %bitcast.119), kind=kOutput, calls=%fused_computation.65 | convolution fusion | flops 201326592 | bytes 33628160 | tf_op jit(solution)/shard_map/while/body/eval_jaxpr/while/body/eval_jaxpr/dot_general | solution.py:25
  300.7 14.0 %all-gather.6 = f32[8,2,1024]{2,1,0:T(2,128)S(1)} all-gather(f32[1,2,1024]{2,1,0:T(2,128)S(1)} %maximum_bitcast_fusion.1), channel_id=4, replica_groups=mesh['freq'=4,'rows'=8] {'rows'}, dimensions={0}, use_global_device_ids=true | all-gather | bytes 73728 | tf_op jit(solution)/shard_map/while/body/eval_jaxpr/all_gather | solution.py:45
  314.7 0.7 multiply_reduce_fusion.1
  316.1 32.2 %fusion.10 = f32[1024,2]{0,1:T(2,128)S(1)} fusion(f32[1024,8192]{1,0:T(8,128)} %get-tuple-element.182, f32[2,8192]{1,0:T(2,128)S(1)} %bitcast.120), kind=kOutput, calls=%fused_computation.68 | convolution fusion | flops 201326592 | bytes 33628160 | tf_op jit(solution)/shard_map/while/body/eval_jaxpr/while/body/eval_jaxpr/dot_general | solution.py:28
  348.3 31.7 %fusion.9 = f32[1024,2]{0,1:T(2,128)S(1)} fusion(f32[1024,8192]{1,0:T(8,128)} %get-tuple-element.181, f32[2,8192]{1,0:T(2,128)S(1)} %bitcast.121), kind=kOutput, calls=%fused_computation.67 | convolution fusion | flops 201326592 | bytes 33628160 | tf_op jit(solution)/shard_map/while/body/eval_jaxpr/while/body/eval_jaxpr/dot_general | solution.py:25
  380.1 14.0 %all-gather.7 = f32[8,2,1024]{2,1,0:T(2,128)S(1)} all-gather(f32[1,2,1024]{2,1,0:T(2,128)S(1)} %maximum_bitcast_fusion.2), channel_id=5, replica_groups=mesh['freq'=4,'rows'=8] {'rows'}, dimensions={0}, use_global_device_ids=true | all-gather | bytes 73728 | tf_op jit(solution)/shard_map/while/body/eval_jaxpr/all_gather | solution.py:45
  394.1 0.7 multiply_reduce_fusion
  395.5 31.9 %fusion.12 = f32[1024,2]{0,1:T(2,128)S(1)} fusion(f32[1024,8192]{1,0:T(8,128)} %get-tuple-element.182, f32[2,8192]{1,0:T(2,128)S(1)} %bitcast.113), kind=kOutput, calls=%fused_computation.70 | convolution fusion | flops 201326592 | bytes 33628160 | tf_op jit(solution)/shard_map/while/body/eval_jaxpr/while/body/eval_jaxpr/dot_general | solution.py:28
  427.4 31.7 %fusion.11 = f32[1024,2]{0,1:T(2,128)S(1)} fusion(f32[1024,8192]{1,0:T(8,128)} %get-tuple-element.181, f32[2,8192]{1,0:T(2,128)S(1)} %bitcast.114), kind=kOutput, calls=%fused_computation.69 | convolution fusion | flops 201326592 | bytes 33628160 | tf_op jit(solution)/shard_map/while/body/eval_jaxpr/while/body/eval_jaxpr/dot_general | solution.py:25
  459.2 14.0 %all-gather.8 = f32[8,2,1024]{2,1,0:T(2,128)S(1)} all-gather(f32[1,2,1024]{2,1,0:T(2,128)S(1)} %maximum_bitcast_fusion.3), channel_id=6, replica_groups=mesh['freq'=4,'rows'=8] {'rows'}, dimensions={0}, use_global_device_ids=true | all-gather | bytes 73728 | tf_op jit(solution)/shard_map/while/body/eval_jaxpr/all_gather | solution.py:45
  473.2 0.7 fusion.4
  474.6 0.6 maximum_divide_fusion.3
  475.2 0.8 add_reduce_fusion
  476.0 1.8 maximum_multiply_fusion
  (19 shorter events, 0.3 us)
